TPU v7x, 128 devices: a whole 4x4x4 slice. The times are simulated.
128 devices in a mesh: gx: 8 (over y_lo, z), gy: 4 (over x), gz: 4 (over y_hi, core).
Axes of the slice: x: 4, y: 4 (y_hi: 2, y_lo: 2; y = y_hi * 2 + y_lo), z: 4, core: 2. Of those that a mesh axis runs over, the one named last changes fastest.
Arguments:
- snapshots: float32 [4, 4, 4096, 8192], P(None, 'gz', 'gx', 'gy'), may hold values from -6 to 6
- steps: int32 [4], replicated, may hold values from 0 to 3999
- mask: int32 [4, 64], replicated, may hold values 0 or 1
- probe: float32 [4096], replicated, may hold values from -6 to 6
Outputs:
- weights: bfloat16 [4, 4096, 8192], P(None, ('gx', 'gy'), 'gz')
- checks: float32 [4, 64], replicated
All inputs are finite; a program needn't handle non-finite values.
Results may differ from a plain program's by a relative error of at most 0.0029.
Values may be sent and summed in bfloat16 or wider, within the bound.
No kernel may reach another device: no remote copies, remote signals or barrier semaphores. Data moves between devices by JAX's collectives and lax.ppermute only.
A program may use at most 128 MiB of HBM per device.

v0:
```python
import functools
import math

import jax
import jax.numpy as jnp
from jax import lax
from jax.sharding import Mesh
from jax.sharding import PartitionSpec as P

D = 4096
BLOCK = 128
GZ = ("gz_0", "gz_1")
GX = ("gx_0", "gx_1")
GX_GY_GZ = ("gx_0", "gx_1", "gy", "gz_0", "gz_1")
GX_GY = ("gx_0", "gx_1", "gy")


decay_span = 1000.0


def over_axes(x, axes):
    return functools.reduce(lax.psum, axes, x)


def blend_coef(steps):
    expo = jnp.exp(steps.astype(jnp.float32) / decay_span)
    return expo / jnp.sum(expo)


def blend_all(stack, coef):
    acc = coef[0] * stack[0]
    for k in range(1, stack.shape[0]):
        acc = acc + coef[k] * stack[k]
    return acc


def apply_mask(blended, mask_part):
    wide_mask = jnp.repeat(mask_part.astype(jnp.float32), BLOCK, axis=1)
    return (blended * wide_mask[:, None, :]).astype(jnp.bfloat16)


def block_checks(weights, probe_rows):
    per_col = jnp.einsum(
        "d,ldc->lc",
        probe_rows,
        weights,
        preferred_element_type=jnp.float32,
        precision=lax.Precision.HIGHEST,
    )
    layer_count = per_col.shape[0]
    grouped = per_col.reshape(layer_count, per_col.shape[1] // BLOCK, BLOCK)
    return jnp.sum(grouped, axis=2) / math.sqrt(D * BLOCK)


def local(snapshots, steps, mask, probe):
    coef = blend_coef(steps)
    layer_total = mask.shape[0]
    block_total = mask.shape[1]
    empty = jnp.zeros((layer_total, block_total), jnp.float32)
    layer_count = snapshots.shape[1]
    row_count = snapshots.shape[2]
    block_count = snapshots.shape[3] // BLOCK
    layer_start = lax.axis_index(GZ) * layer_count
    col_start = lax.axis_index("gy") * block_count
    mask_part = lax.dynamic_slice(mask, (layer_start, col_start), (layer_count, block_count))
    local_weights = apply_mask(blend_all(snapshots, coef), mask_part)
    probe_rows = lax.dynamic_slice_in_dim(probe, lax.axis_index(GX) * row_count, row_count, 0)
    partial_checks = block_checks(local_weights, probe_rows)
    placed = lax.dynamic_update_slice(empty, partial_checks, (layer_start, col_start))
    weights = lax.all_to_all(
        lax.all_to_all(local_weights, "gy", split_axis=1, concat_axis=2, tiled=True),
        GZ,
        split_axis=2,
        concat_axis=0,
        tiled=True,
    )
    checks = over_axes(placed, GX_GY_GZ)
    return (weights, checks)


def solution(mesh):
    split = Mesh(
        mesh.devices.reshape(2, 4, mesh.shape["gy"], 2, 2), ("gx_0", "gx_1", "gy", "gz_0", "gz_1")
    )
    placed = (P(None, GZ, GX, "gy"), P(), P(), P())
    return jax.shard_map(
        local, mesh=split, in_specs=placed, out_specs=(P(None, GX_GY, GZ), P()), check_vma=False
    )
```

profile of v0, /device:TPU:1, one launch (start us, length us, event | category | flops | bytes accessed | tf_op | source)
XLA Modules:
  0.0 223.8 jit_solution(7648449169026337634)
XLA Ops:
  0.6 0.0 copy-start
  0.7 0.8 convert_bitcast_fusion
  1.4 0.1 broadcast_bitcast_fusion
  1.5 6.5 %fusion.11 = (f32[1,1,512,2048]{3,2,1,0:T(8,128)S(1)}, f32[1,1,512,2048]{3,2,1,0:T(8,128)S(1)}, f32[1,1,512,2048]{3,2,1,0:T(8,128)S(1)}, f32[1,1,512,2048]{3,2,1,0:T(8,128)S(1)}) fusion(f32[4,1,512,2048]{3,2,1,0:T(8,128)} %param.4), kind=kLoop, calls=%fused_computation.21 | loop fusion | bytes 33554432 | tf_op jit(solution)/shard_map/slice | solution.py:31
  8.0 0.6 fusion.9
  8.6 0.7 broadcast_divide_fusion
  9.2 0.6 fusion.12
  9.8 33.7 %fusion.4 = (bf16[1,512,2048]{2,0,1:T(2,128)(2,1)}, f32[1,1,512,2048]{3,0,2,1:T(1,128)}) fusion(f32[2048]{0:T(1024)S(1)} %broadcast_bitcast_fusion, f32[1,1,512,2048]{3,2,1,0:T(8,128)S(1)} %get-tuple-element.15, f32[]{:T(128)} %bitcast.3, f32[1,1,512,2048]{3,2,1,0:T(8,128)S(1)} %get-tuple-element.13, f32[]{:T(128)} %bitcast.2, ...), kind=kLoop, calls=%fused_computation.10 | loop fusion | flops 9437184 | bytes 23076880 | tf_op jit(solution)/shard_map/convert_element_type | solution.py:39
  43.6 0.5 broadcast.106
  44.1 13.2 %reduce.2 = bf16[512,2048]{1,0:T(8,128)(2,1)S(1)} reduce(bf16[512,1,2048]{2,1,0:T(2,128)(2,1)} %bitcast.52, bf16[]{:T(256)} %broadcast.106), dimensions={1}, to_apply=%bitcast.38.reduce_sub_computation | reduce | bytes 4194306
  57.3 2.8 %reshape.158 = bf16[4,2,131072]{2,1,0:T(2,128)(2,1)} reshape(bf16[512,2048]{1,0:T(8,128)(2,1)S(1)} %reduce.2) | data formatting | bytes 4194304
  60.0 30.3 %all_to_all.36 = bf16[4,2,131072]{2,1,0:T(2,128)(2,1)S(1)} all-to-all(bf16[4,2,131072]{2,1,0:T(2,128)(2,1)} %reshape.158), channel_id=1, replica_groups=mesh['gx_0'=2,'gx_1'=4,'gy'=4,'gz_0'=2,'gz_1'=2] {'gy'}, dimensions={0} | all-to-all | bytes 4194304 | tf_op jit(solution)/shard_map/all_to_all | solution.py:71
  90.3 3.3 %reshape.159 = bf16[512,1,2048]{2,1,0:T(2,128)(2,1)} reshape(bf16[4,2,131072]{2,1,0:T(2,128)(2,1)S(1)} %all_to_all.36) | data formatting | bytes 4194304
  93.7 3.5 %copy.25 = bf16[1,512,2048]{2,1,0:T(8,128)(2,1)S(1)} copy(bf16[1,512,2048]{2,0,1:T(2,128)(2,1)} %bitcast.50) | data formatting | bytes 4194304
  97.1 2.5 %copy.20 = bf16[1,128,4,2048]{1,3,2,0:T(8,128)(2,1)} copy(bf16[1,128,4,2048]{3,1,2,0:T(8,128)(2,1)S(1)} %bitcast.53) | data formatting | bytes 4194304 | tf_op jit(solution)/shard_map/all_to_all | solution.py:71
  99.6 7.5 %copy.63 = bf16[1,128,8192]{1,0,2:T(2,128)(2,1)} copy(bf16[1,128,8192]{1,2,0:T(8,128)(2,1)} %bitcast.54) | data formatting | bytes 4194304 | tf_op jit(solution)/shard_map/all_to_all | solution.py:71
  107.1 45.2 %reduce.3 = bf16[8192,128]{1,0:T(8,128)(2,1)S(1)} reduce(bf16[8192,1,128]{2,1,0:T(2,128)(2,1)} %bitcast.49, bf16[]{:T(256)} %broadcast.106), dimensions={1}, to_apply=%bitcast.48.reduce_sub_computation | reduce | bytes 4194306
  152.3 2.1 reshape.160
  154.3 6.3 %all-to-all-start.1 = ((bf16[4,2,131072]{2,1,0:T(2,128)(2,1)}), bf16[4,2,131072]{2,1,0:T(2,128)(2,1)S(1)}, u32[]{:S(2)}, u32[]{:S(2)}) async-start(bf16[4,2,131072]{2,1,0:T(2,128)(2,1)} %reshape.160), calls=%async_computation.1 | async-start | bytes 4194304 | tf_op jit(solution)/shard_map/all_to_all | solution.py:70
  160.6 0.1 dynamic_slice.7
  160.7 4.1 %fusion.6 = f32[1,16,128]{2,0,1:T(1,128)S(1)} fusion(f32[512,1,1]{0,1,2:T(1,128)S(1)} %bitcast.57, f32[1,1,512,2048]{3,0,2,1:T(1,128)} %get-tuple-element.11, f32[2048]{0:T(1024)S(1)} %broadcast_bitcast_fusion), kind=kOutput, calls=%fused_computation.12 | convolution fusion | flops 14680064 | bytes 4212736 | tf_op jit(solution)/shard_map/d,ldc->lc/dot_general | solution.py:43
  164.7 0.1 reduce_sum.19
  164.9 0.2 dynamic_update_slice.3
  165.0 19.8 %psum.35 = f32[4,64]{1,0:T(4,128)S(1)} all-reduce(f32[4,64]{1,0:T(4,128)S(1)} %dynamic_update_slice.3), channel_id=1, replica_groups=mesh['gx_0'=2,'gx_1'=4,'gy'=4,'gz_0'=2,'gz_1'=2] {'gx_0'}, use_global_device_ids=true, to_apply=%region_2.0 | all-reduce | flops 256 | bytes 2048 | tf_op jit(solution)/shard_map/psum | solution.py:22
  184.8 9.7 %psum.36 = f32[4,64]{1,0:T(4,128)S(1)} all-reduce(f32[4,64]{1,0:T(4,128)S(1)} %psum.35), channel_id=1, replica_groups=mesh['gx_0'=2,'gx_1'=4,'gy'=4,'gz_0'=2,'gz_1'=2] {'gx_1'}, use_global_device_ids=true, to_apply=%region_3.0 | all-reduce | flops 256 | bytes 2048 | tf_op jit(solution)/shard_map/psum | solution.py:22
  194.5 6.9 %psum.37 = f32[4,64]{1,0:T(4,128)S(1)} all-reduce(f32[4,64]{1,0:T(4,128)S(1)} %psum.36), channel_id=1, replica_groups=mesh['gx_0'=2,'gx_1'=4,'gy'=4,'gz_0'=2,'gz_1'=2] {'gy'}, use_global_device_ids=true, to_apply=%region_4.0 | all-reduce | flops 256 | bytes 2048 | tf_op jit(solution)/shard_map/psum | solution.py:22
  201.4 5.3 %psum.38 = f32[4,64]{1,0:T(4,128)S(1)} all-reduce(f32[4,64]{1,0:T(4,128)S(1)} %psum.37), channel_id=1, replica_groups=mesh['gx_0'=2,'gx_1'=4,'gy'=4,'gz_0'=2,'gz_1'=2] {'gz_0'}, use_global_device_ids=true, to_apply=%region_5.0 | all-reduce | flops 256 | bytes 2048 | tf_op jit(solution)/shard_map/psum | solution.py:22
  206.7 8.7 %psum.39 = f32[4,64]{1,0:T(4,128)} all-reduce(f32[4,64]{1,0:T(4,128)S(1)} %psum.38), channel_id=1, replica_groups=mesh['gx_0'=2,'gx_1'=4,'gy'=4,'gz_0'=2,'gz_1'=2] {'gz_1'}, use_global_device_ids=true, to_apply=%region_6.0 | all-reduce | flops 256 | bytes 2048 | tf_op jit(solution)/shard_map/psum | solution.py:22
  215.3 0.0 all-to-all-done.1
  215.3 3.4 %reshape.161 = bf16[8192,1,128]{2,1,0:T(2,128)(2,1)} reshape(bf16[4,2,131072]{2,1,0:T(2,128)(2,1)S(1)} %all-to-all-done.1) | data formatting | bytes 4194304
  218.7 2.5 %copy.26 = bf16[1,128,8192]{1,2,0:T(8,128)(2,1)S(1)} copy(bf16[1,128,8192]{1,0,2:T(2,128)(2,1)} %bitcast.51) | data formatting | bytes 4194304
  221.2 2.6 %copy.22 = bf16[4,128,2048]{2,1,0:T(8,128)(2,1)} copy(bf16[4,128,2048]{1,2,0:T(8,128)(2,1)S(1)} %bitcast.55) | data formatting | bytes 4194304
  (5 shorter events, 0.0 us)
Async XLA Ops:
  0.6 160.0 %copy-start = (f32[4096]{0:T(1024)S(1)}, f32[4096]{0:T(1024)}, u32[]{:S(2)}) copy-start(f32[4096]{0:T(1024)} %param.7) | copy-start | bytes 49156
  1.5 6.5 %copy-start.1 = (s32[4]{0:T(128)S(1)}, s32[4]{0:T(128)}, u32[]{:S(2)}) copy-start(s32[4]{0:T(128)} %param.5) | copy-start | bytes 52
  154.3 61.0 %all-to-all-start.1 = ((bf16[4,2,131072]{2,1,0:T(2,128)(2,1)}), bf16[4,2,131072]{2,1,0:T(2,128)(2,1)S(1)}, u32[]{:S(2)}, u32[]{:S(2)}) async-start(bf16[4,2,131072]{2,1,0:T(2,128)(2,1)} %reshape.160), calls=%async_computation.1 | async-start | bytes 4194304 | tf_op jit(solution)/shard_map/all_to_all | solution.py:70
where the time goes:
time: 225 us; the launch traced here: 224 us
  other arithmetic  94.2 us (42%)
  blocking collectives  80.6 us (36%)
  local copies, waits for them, and re-layouts  37.9 us (17%)
  starting transfers between devices  6.27 us (3%)
  matrix products  4.07 us (2%)
    unnamed x2, other arithmetic  58.3 us
    psum x5, blocking collectives, over_axes(): return functools.reduce(lax.psum, axes, x)  50.3 us
    convert_element_type x1, other arithmetic, apply_mask(): return (blended * wide_mask[:, None, :]).astype(jnp.bfloat16)  33.7 us
    all_to_all x1, blocking collectives, local(): lax.all_to_all(local_weights, 'gy', split_axis=1, concat_axis=2, tiled=True)  30.3 us
    unnamed x12, local copies, waits for them, and re-layouts  20.5 us
    all_to_all x2, local copies, waits for them, and re-layouts, local(): lax.all_to_all(local_weights, 'gy', split_axis=1, concat_axis=2, tiled=True)  9.96 us
    slice x2, local copies, waits for them, and re-layouts, blend_all(): acc = coef[0] * stack[0]  7.07 us
    all_to_all x1, starting transfers between devices, local(): lax.all_to_all(lax.all_to_all(local_weights, 'gy', split_axis=1, concat_a...  6.27 us
  transfers between devices with their start and end apart: 1, of which 0 were waited for; matrix products, arithmetic and copies ran while one was open for 2% of the time, Pallas kernels for 0%

commit v1 on v0

v1 whole, which is shorter than its diff:
```python
import functools
import math

import jax
import jax.numpy as jnp
from jax import lax
from jax.experimental import pallas as pl
from jax.experimental.pallas import tpu as pltpu
from jax.sharding import PartitionSpec as P

BLOCK = 128
DECAY_SPAN = 1000.0
ORDER = (2, 1, 3, 0)
ROWS_PER_STEP = 32
AXES = ("gx", "gy", "gz")


def blend_step(shift, first, last, steps, mask, x_ref, p_ref, part_in, w_ref, part_out, pcol, acc):
    i = pl.program_id(0)
    n = pl.num_programs(0)
    rs = x_ref.shape[2]
    nblk = x_ref.shape[3] // BLOCK
    gy = lax.axis_index("gy")
    gz = lax.axis_index("gz")
    gx = lax.axis_index("gx")
    rows = pcol.shape[0]

    @pl.when(i == 0)
    def _():
        row = gx * 4 + lax.rem(gz + shift, 4)
        pcol[...] = jnp.broadcast_to(p_ref[pl.ds(row, 1), :], (rows, BLOCK)).T
        if first:
            acc[...] = jnp.zeros_like(acc)
        else:
            acc[...] = part_in[...]

    expo = [
        jnp.exp(jnp.full((8, BLOCK), steps[k].astype(jnp.float32), jnp.float32) / DECAY_SPAN)
        for k in range(4)
    ]
    total = ((expo[0] + expo[1]) + expo[2]) + expo[3]
    coef = [jnp.broadcast_to((e / total)[None], (rs // 8, 8, BLOCK)).reshape(rs, BLOCK) for e in expo]
    probe = pcol[pl.ds(pl.multiple_of(i * rs, rs), rs), :]
    for b in range(nblk):
        cols = slice(b * BLOCK, (b + 1) * BLOCK)
        out = coef[0] * x_ref[0, 0, :, cols]
        for k in range(1, 4):
            out = out + coef[k] * x_ref[k, 0, :, cols]
        on = mask[gz, gy * nblk + b].astype(jnp.float32)
        w = (out * on).astype(jnp.bfloat16)
        w_ref[:, cols] = w
        term = probe * w.astype(jnp.float32)
        acc[b * 8 : (b + 1) * 8, :] += jnp.sum(term.reshape(rs // 8, 8, BLOCK), axis=0)

    @pl.when(i == n - 1)
    def _():
        if last:
            pcol[...] = jnp.zeros_like(pcol)
            lanes = jnp.sum(acc[...].reshape(nblk, 8, BLOCK), axis=1)
            pcol[pl.ds(pl.multiple_of(gy * nblk, nblk), nblk), :] = lanes
            mine = jnp.sum(pcol[...].T, axis=0, keepdims=True)
            part_out[...] = jnp.broadcast_to(mine, part_out.shape)
        else:
            part_out[...] = acc[...]


def blend(index, snapshots, steps, mask, probe, part):
    shift = ORDER[index]
    first, last = index == 0, index == len(ORDER) - 1
    snaps, _, rows, cols = snapshots.shape
    sub = rows // 4
    grid = sub // ROWS_PER_STEP

    def rowblock(i):
        return lax.rem(lax.axis_index("gz") + shift, 4) * grid + i

    whole = lambda i: (0, 0)
    part_shape = (128, BLOCK)
    ins = [
        pl.BlockSpec(memory_space=pltpu.SMEM),
        pl.BlockSpec(memory_space=pltpu.SMEM),
        pl.BlockSpec((snaps, 1, ROWS_PER_STEP, cols), lambda i: (0, 0, rowblock(i), 0)),
        pl.BlockSpec((32, BLOCK), whole),
    ]
    args = [steps, mask, snapshots, probe]
    if first:
        body = lambda st, mk, x, p, w, po, pc, ac: blend_step(shift, True, last, st, mk, x, p, None, w, po, pc, ac)
    else:
        body = functools.partial(blend_step, shift, False, last)
        ins.append(pl.BlockSpec(part_shape, whole))
        args.append(part)
    return pl.pallas_call(
        body,
        grid=(grid,),
        in_specs=ins,
        out_specs=[
            pl.BlockSpec((ROWS_PER_STEP, cols), lambda i: (i, 0)),
            pl.BlockSpec(part_shape, whole),
        ],
        out_shape=[
            jax.ShapeDtypeStruct((sub, cols), jnp.bfloat16),
            jax.ShapeDtypeStruct(part_shape, jnp.float32),
        ],
        scratch_shapes=[pltpu.VMEM((sub, BLOCK), jnp.float32), pltpu.VMEM((128, BLOCK), jnp.float32)],
        cost_estimate=pl.CostEstimate(
            flops=12 * sub * cols, bytes_accessed=snaps * sub * cols * 4 + sub * cols * 2, transcendentals=0
        ),
        name=f"blend{index}",
    )(*args)


def finish_kernel(got0, got1, got2, got3, parts, out, checks, sems):
    gy = lax.axis_index("gy")
    copies = []
    for j, got in enumerate((got0, got1, got2, got3)):
        slot = lax.rem(gy + 4 - ORDER[j], 4)
        copy = pltpu.make_async_copy(got, out.at[slot], sems.at[j])
        copy.start()
        copies.append(copy)
    t = jnp.sum(parts[...].reshape(16, 8, BLOCK), axis=0)
    checks[...] = (t[0:4] + t[4:8])[:, 0:64] / math.sqrt(4096 * BLOCK)
    for copy in copies:
        copy.wait()


def finish(got, parts):
    sub, cols = got[0].shape
    vmem = pl.BlockSpec(memory_space=pltpu.VMEM)
    return pl.pallas_call(
        finish_kernel,
        in_specs=[vmem] * 5,
        out_specs=[pl.BlockSpec(memory_space=pl.ANY), vmem],
        out_shape=[
            jax.ShapeDtypeStruct((4, sub, cols), jnp.bfloat16),
            jax.ShapeDtypeStruct((4, 64), jnp.float32),
        ],
        scratch_shapes=[pltpu.SemaphoreType.DMA((4,))],
        name="finish",
    )(*got, parts)


def route(shift):
    pairs = []
    for gx in range(8):
        for gy in range(4):
            for gz in range(4):
                pairs.append((gx * 16 + gy * 4 + gz, gx * 16 + ((gz + shift) % 4) * 4 + gy))
    return pairs


def local(snapshots, steps, mask, probe):
    probe = probe.reshape(32, BLOCK)
    part = None
    got = []
    for index, shift in enumerate(ORDER):
        w, part = blend(index, snapshots, steps, mask, probe, part)
        got.append(lax.ppermute(w, AXES, route(shift)))
    parts = lax.all_to_all(part, AXES, 0, 0, tiled=True)
    return tuple(finish(got, parts))


def solution(mesh):
    return jax.shard_map(
        local,
        mesh=mesh,
        in_specs=(P(None, "gz", "gx", "gy"), P(), P(), P()),
        out_specs=(P(None, ("gx", "gy"), "gz"), P()),
        check_vma=False,
    )
```

time: 225 us -> 57.5 us (0.26)
  other arithmetic: 94.2 us -> 0 us
  blocking collectives: 80.6 us -> 24.2 us
  local copies, waits for them, and re-layouts: 37.9 us -> 1.27 us
  Pallas kernels: 0 us -> 20.8 us
  matrix products: 4.07 us -> 0 us
  starting transfers between devices: 6.27 us -> 9.99 us
    unnamed x2 -> x0, other arithmetic: 58.3 us -> none
    psum x5 -> x0, blocking collectives: 50.3 us -> none  [over_axes(): return functools.reduce(lax.psum, axes, x)]
    convert_element_type x2 -> x0, other arithmetic: 34.5 us -> none  [the longest x1 33.7 us: apply_mask(): return (blended * wide_mask[:, None, :]).astype(jnp.bfloat16)]
    pallas_call x0 -> x5, Pallas kernels: none -> 20.8 us  [the longest x4 17.3 us: blend(): pl.pallas_call(body, grid=(grid,), in_specs=ins, out_specs=[pl.BlockSpec(...]
    unnamed x12 -> x8, local copies, waits for them, and re-layouts: 20.5 us -> 1.27 us
    ppermute x0 -> x4, starting transfers between devices: none -> 9.99 us  [local(): got.append(lax.ppermute(w, AXES, route(shift)))]
    all_to_all x2 -> x0, local copies, waits for them, and re-layouts: 9.96 us -> none  [local(): lax.all_to_all(local_weights, 'gy', split_axis=1, concat_axis=2, tiled=True)]
    slice x2 -> x0, local copies, waits for them, and re-layouts: 7.07 us -> none  [blend_all(): acc = coef[0] * stack[0]]
  transfers between devices with their start and end apart: 1 -> 4, of which waited for: 0 -> 0; matrix products, arithmetic and copies ran while one was open for 2% -> 0% of each run, Pallas kernels for 0% -> 23%
where the time goes in v1:
time: 57.5 us; the launch traced here: 56.9 us
  blocking collectives  24.2 us (42%)
  Pallas kernels  20.8 us (36%)
  starting transfers between devices  9.99 us (17%)
  local copies, waits for them, and re-layouts  1.27 us (2%)
  between operations  0.69 us (1%)
    all_to_all x1, blocking collectives, local(): parts = lax.all_to_all(part, AXES, 0, 0, tiled=True)  24.2 us
    pallas_call x4, Pallas kernels, blend(): pl.pallas_call(body, grid=(grid,), in_specs=ins, out_specs=[pl.BlockSpec(...  17.3 us
    ppermute x4, starting transfers between devices, local(): got.append(lax.ppermute(w, AXES, route(shift)))  9.99 us
    pallas_call x1, Pallas kernels, finish(): pl.pallas_call(finish_kernel, in_specs=[vmem] * 5, out_specs=[pl.BlockSpe...  3.45 us
    unnamed x8, local copies, waits for them, and re-layouts  1.27 us
  transfers between devices with their start and end apart: 4, of which 0 were waited for; matrix products, arithmetic and copies ran while one was open for 0% of the time, Pallas kernels for 23%

profile of v1, /device:TPU:1, one launch (start us, length us, event | category | flops | bytes accessed | tf_op | source)
XLA Modules:
  0.0 56.9 jit_solution(18146139978366201810)
XLA Ops:
  0.6 4.3 %blend0.1 = (bf16[128,2048]{1,0:T(8,128)(2,1)}, f32[128,128]{1,0:T(8,128)}) custom-call(s32[4]{0:T(128)} %steps.5, s32[4,64]{1,0:T(4,128)} %mask.5, f32[4,1,512,2048]{3,2,1,0:T(8,128)} %x_ref.5, f32[32,128]{1,0:T(8,128)} %bitcast.5), custom_call_target="tpu_custom_call" | custom-call | flops 3145728 | bytes 4718592 | tf_op jit(solution)/shard_map/blend0/pallas_call | solution.py:92
  4.9 3.9 %collective-permute-start = (bf16[128,2048]{1,0:T(8,128)(2,1)}, bf16[128,2048]{1,0:T(8,128)(2,1)S(1)}, u32[]{:S(2)}, u32[]{:S(2)}) collective-permute-start(bf16[128,2048]{1,0:T(8,128)(2,1)} %get-tuple-element.10), channel_id=1, source_target_pairs={{0,8},{1,12},{2,0},{3,4},{4,9},{5,13},{6,1},{7,5},{8,10},{9,14},{1... | collective-permute-start | bytes 1572872 | tf_op jit(solution)/shard_map/ppermute | solution.py:157
  8.8 4.3 %blend1.1 = (bf16[128,2048]{1,0:T(8,128)(2,1)}, f32[128,128]{1,0:T(8,128)}) custom-call(s32[4]{0:T(128)} %steps.5, s32[4,64]{1,0:T(4,128)} %mask.5, f32[4,1,512,2048]{3,2,1,0:T(8,128)} %x_ref.5, f32[32,128]{1,0:T(8,128)} %bitcast.6, f32[128,128]{1,0:T(8,128)} %get-tuple-element.11.part_in), custom_call_target="tpu_custom_call" | custom-call | flops 3145728 | bytes 4718592 | tf_op jit(solution)/shard_map/blend1/pallas_call | solution.py:92
  13.1 3.5 %collective-permute-start.1 = (bf16[128,2048]{1,0:T(8,128)(2,1)}, bf16[128,2048]{1,0:T(8,128)(2,1)S(1)}, u32[]{:S(2)}, u32[]{:S(2)}) collective-permute-start(bf16[128,2048]{1,0:T(8,128)(2,1)} %get-tuple-element.12), channel_id=1, source_target_pairs={{0,4},{1,8},{2,12},{3,0},{4,5},{5,9},{6,13},{7,1},{8,6},{9,10},{10... | collective-permute-start | bytes 1572872 | tf_op jit(solution)/shard_map/ppermute | solution.py:157
  16.5 4.3 %blend2.1 = (bf16[128,2048]{1,0:T(8,128)(2,1)}, f32[128,128]{1,0:T(8,128)}) custom-call(s32[4]{0:T(128)} %steps.5, s32[4,64]{1,0:T(4,128)} %mask.5, f32[4,1,512,2048]{3,2,1,0:T(8,128)} %x_ref.5, f32[32,128]{1,0:T(8,128)} %bitcast.7, f32[128,128]{1,0:T(8,128)} %get-tuple-element.13.part_in), custom_call_target="tpu_custom_call" | custom-call | flops 3145728 | bytes 4718592 | tf_op jit(solution)/shard_map/blend2/pallas_call | solution.py:92
  20.8 0.0 collective-permute-start.2
  20.8 4.4 %blend3.1 = (bf16[128,2048]{1,0:T(8,128)(2,1)}, f32[128,128]{1,0:T(8,128)}) custom-call(s32[4]{0:T(128)} %steps.5, s32[4,64]{1,0:T(4,128)} %mask.5, f32[4,1,512,2048]{3,2,1,0:T(8,128)} %x_ref.5, f32[32,128]{1,0:T(8,128)} %bitcast.8, f32[128,128]{1,0:T(8,128)} %get-tuple-element.15.part_in), custom_call_target="tpu_custom_call" | custom-call | flops 3145728 | bytes 4718592 | tf_op jit(solution)/shard_map/blend3/pallas_call | solution.py:92
  25.3 2.7 %collective-permute-start.3 = (bf16[128,2048]{1,0:T(8,128)(2,1)}, bf16[128,2048]{1,0:T(8,128)(2,1)S(1)}, u32[]{:S(2)}, u32[]{:S(2)}) collective-permute-start(bf16[128,2048]{1,0:T(8,128)(2,1)} %get-tuple-element.16), channel_id=1, source_target_pairs={{0,0},{1,4},{2,8},{3,12},{4,1},{5,5},{6,9},{7,13},{8,2},{9,6},{10,... | collective-permute-start | bytes 1572872 | tf_op jit(solution)/shard_map/ppermute | solution.py:157
  28.0 24.2 %all_to_all.11 = f32[128,1,128]{2,1,0:T(1,128)} all-to-all(f32[128,1,128]{2,1,0:T(1,128)} %bitcast.10), channel_id=1, replica_groups=mesh['gx'=8,'gy'=4,'gz'=4] {'gx','gy','gz'}, dimensions={0} | all-to-all | bytes 131072 | tf_op jit(solution)/shard_map/all_to_all | solution.py:158
  52.2 0.0 collective-permute-done.got0
  52.2 0.0 copy-start
  52.2 0.0 collective-permute-done.1.got1
  52.2 0.0 copy-start.1
  52.2 0.0 collective-permute-done.2.got2
  52.2 0.0 copy-start.2
  52.2 0.0 collective-permute-done.3.got3
  52.2 0.0 copy-start.3
  52.2 0.7 %copy-done = bf16[128,2048]{1,0:T(8,128)(2,1)} copy-done((bf16[128,2048]{1,0:T(8,128)(2,1)}, bf16[128,2048]{1,0:T(8,128)(2,1)S(1)}, u32[]{:S(2)}) %copy-start) | copy-done | bytes 524312
  53.0 0.2 copy-done.1
  53.1 0.2 copy-done.2
  53.3 0.2 copy-done.3
  53.5 3.5 %finish.1 = (bf16[4,128,2048]{2,1,0:T(8,128)(2,1)}, f32[4,64]{1,0:T(4,128)}) custom-call(bf16[128,2048]{1,0:T(8,128)(2,1)} %copy-done, bf16[128,2048]{1,0:T(8,128)(2,1)} %copy-done.1, bf16[128,2048]{1,0:T(8,128)(2,1)} %copy-done.2, bf16[128,2048]{1,0:T(8,128)(2,1)} %copy-done.3, f32[128,128]{1,0:T(8,128)} %bitcast.9), custom_call_target="tpu_custom_call" | custom-call | tf_op jit(solution)/shard_map/finish/pallas_call | solution.py:129
Async XLA Ops:
  4.9 47.2 %collective-permute-start = (bf16[128,2048]{1,0:T(8,128)(2,1)}, bf16[128,2048]{1,0:T(8,128)(2,1)S(1)}, u32[]{:S(2)}, u32[]{:S(2)}) collective-permute-start(bf16[128,2048]{1,0:T(8,128)(2,1)} %get-tuple-element.10), channel_id=1, source_target_pairs={{0,8},{1,12},{2,0},{3,4},{4,9},{5,13},{6,1},{7,5},{8,10},{9,14},{1... | collective-permute-start | bytes 1572872 | tf_op jit(solution)/shard_map/ppermute | solution.py:157
  13.1 39.1 %collective-permute-start.1 = (bf16[128,2048]{1,0:T(8,128)(2,1)}, bf16[128,2048]{1,0:T(8,128)(2,1)S(1)}, u32[]{:S(2)}, u32[]{:S(2)}) collective-permute-start(bf16[128,2048]{1,0:T(8,128)(2,1)} %get-tuple-element.12), channel_id=1, source_target_pairs={{0,4},{1,8},{2,12},{3,0},{4,5},{5,9},{6,13},{7,1},{8,6},{9,10},{10... | collective-permute-start | bytes 1572872 | tf_op jit(solution)/shard_map/ppermute | solution.py:157
  20.8 31.3 %collective-permute-start.2 = (bf16[128,2048]{1,0:T(8,128)(2,1)}, bf16[128,2048]{1,0:T(8,128)(2,1)S(1)}, u32[]{:S(2)}, u32[]{:S(2)}) collective-permute-start(bf16[128,2048]{1,0:T(8,128)(2,1)} %get-tuple-element.14), channel_id=1, source_target_pairs={{0,12},{1,0},{2,4},{3,8},{4,13},{5,1},{6,5},{7,9},{8,14},{9,2},{10... | collective-permute-start | bytes 1572872 | tf_op jit(solution)/shard_map/ppermute | solution.py:157
  25.3 26.9 %collective-permute-start.3 = (bf16[128,2048]{1,0:T(8,128)(2,1)}, bf16[128,2048]{1,0:T(8,128)(2,1)S(1)}, u32[]{:S(2)}, u32[]{:S(2)}) collective-permute-start(bf16[128,2048]{1,0:T(8,128)(2,1)} %get-tuple-element.16), channel_id=1, source_target_pairs={{0,0},{1,4},{2,8},{3,12},{4,1},{5,5},{6,9},{7,13},{8,2},{9,6},{10,... | collective-permute-start | bytes 1572872 | tf_op jit(solution)/shard_map/ppermute | solution.py:157
  52.2 0.8 %copy-start = (bf16[128,2048]{1,0:T(8,128)(2,1)}, bf16[128,2048]{1,0:T(8,128)(2,1)S(1)}, u32[]{:S(2)}) copy-start(bf16[128,2048]{1,0:T(8,128)(2,1)S(1)} %collective-permute-done.got0) | copy-start | bytes 1572868
  52.2 1.0 %copy-start.1 = (bf16[128,2048]{1,0:T(8,128)(2,1)}, bf16[128,2048]{1,0:T(8,128)(2,1)S(1)}, u32[]{:S(2)}) copy-start(bf16[128,2048]{1,0:T(8,128)(2,1)S(1)} %collective-permute-done.1.got1) | copy-start | bytes 1572868
  52.2 1.1 %copy-start.2 = (bf16[128,2048]{1,0:T(8,128)(2,1)}, bf16[128,2048]{1,0:T(8,128)(2,1)S(1)}, u32[]{:S(2)}) copy-start(bf16[128,2048]{1,0:T(8,128)(2,1)S(1)} %collective-permute-done.2.got2) | copy-start | bytes 1572868
  52.2 1.3 %copy-start.3 = (bf16[128,2048]{1,0:T(8,128)(2,1)}, bf16[128,2048]{1,0:T(8,128)(2,1)S(1)}, u32[]{:S(2)}) copy-start(bf16[128,2048]{1,0:T(8,128)(2,1)S(1)} %collective-permute-done.3.got3) | copy-start | bytes 1572868

commit v2 on v1

v2 whole, which is shorter than its diff:
```python
import functools
import math

import jax
import jax.numpy as jnp
from jax import lax
from jax.experimental import pallas as pl
from jax.experimental.pallas import tpu as pltpu
from jax.sharding import PartitionSpec as P

BLOCK = 128
DECAY_SPAN = 1000.0
GROUPS = ((0, 1), (2, 3))
CHUNK = 32
AXES = ("gx", "gy", "gz")
STAGES = (
    ((1, 3, 0, 2), (2, 0, 3, 1), (1, 3, 0, 2), (2, 0, 3, 1)),
    ((2, 0, 3, 1), (1, 3, 0, 2), (2, 0, 3, 1), (1, 3, 0, 2)),
    ((3, 1, 2, 0), (0, 2, 1, 3), (3, 1, 2, 0), (0, 2, 1, 3)),
    ((0, 2, 1, 3), (3, 1, 2, 0), (0, 2, 1, 3), (3, 1, 2, 0)),
)


def lookup(table, i, j):
    packed = sum(table[m][n] << (2 * (4 * m + n)) for m in range(4) for n in range(4))
    packed = packed - (1 << 32) if packed >= 1 << 31 else packed
    return jnp.bitwise_and(lax.shift_right_logical(jnp.int32(packed), (4 * i + j) * 2), 3)


def sent_to(stage, gy, gz):
    return lookup(STAGES[stage], gy, gz)


def layer_from(stage, gy, gz):
    inverse = [[row.index(r) for r in range(4)] for row in STAGES[stage]]
    return lookup(inverse, gz, gy)


def blend_kernel(stages, first, last, *refs):
    steps_hbm, mask_hbm, probe_hbm, x_hbm = refs[:4]
    refs = refs[4:]
    if not first:
        part_in, refs = refs[0], refs[1:]
    w_refs, refs = refs[: len(stages)], refs[len(stages) :]
    part_out, xbuf, steps, mask, p_ref, pcol, acc, small, sems = refs
    nblk = x_hbm.shape[3] // BLOCK
    sub = x_hbm.shape[2] // 4
    per = sub // CHUNK
    gx, gy, gz = (lax.axis_index(a) for a in AXES)
    quarter = [sent_to(s, gy, gz) for s in stages]

    tables = [
        pltpu.make_async_copy(src, dst, small.at[i])
        for i, (src, dst) in enumerate(((steps_hbm, steps), (probe_hbm, p_ref), (mask_hbm, mask)))
    ]

    def fetch(j, c):
        row = pl.multiple_of(quarter[j] * sub + c * CHUNK, CHUNK)
        here = pl.ds(pl.multiple_of(c * CHUNK, CHUNK), CHUNK)
        return pltpu.make_async_copy(
            x_hbm.at[:, 0, pl.ds(row, CHUNK), :], xbuf.at[j, :, here, :], sems.at[j, c]
        )

    for t in tables:
        t.start()
    for j in range(len(stages)):
        for c in range(per):
            fetch(j, c).start()
    for t in tables:
        t.wait()

    if first:
        acc[...] = jnp.zeros_like(acc)
    else:
        acc[...] = part_in[...]
    expo = [
        jnp.exp(jnp.full((8, BLOCK), steps[k].astype(jnp.float32), jnp.float32) / DECAY_SPAN)
        for k in range(4)
    ]
    total = ((expo[0] + expo[1]) + expo[2]) + expo[3]
    coef = [e / total for e in expo]
    wide = [jnp.broadcast_to(c[None], (CHUNK // 8, 8, BLOCK)).reshape(CHUNK, BLOCK) for c in coef]

    for j in range(len(stages)):
        pcol[j] = jnp.broadcast_to(p_ref[pl.ds(gx * 4 + quarter[j], 1), :], (sub, BLOCK)).T

    for j in range(len(stages)):

        def chunk(c, carry):
            fetch(j, c).wait()
            rows = pl.ds(pl.multiple_of(c * CHUNK, CHUNK), CHUNK)
            probe = pcol[j, rows, :]
            for b in range(nblk):
                cols = slice(b * BLOCK, (b + 1) * BLOCK)
                out = wide[0] * xbuf[j, 0, rows, cols]
                for k in range(1, 4):
                    out = out + wide[k] * xbuf[j, k, rows, cols]
                on = mask[gz, gy * nblk + b].astype(jnp.float32)
                w = (out * on).astype(jnp.bfloat16)
                w_refs[j][rows, cols] = w
                term = probe * w.astype(jnp.float32)
                acc[b * 8 : (b + 1) * 8, :] += jnp.sum(term.reshape(CHUNK // 8, 8, BLOCK), axis=0)
            return carry

        lax.fori_loop(0, per, chunk, 0)

    if last:
        lanes = jnp.sum(acc[...].reshape(nblk, 8, BLOCK), axis=1)
        acc[...] = jnp.zeros_like(acc)
        acc[pl.ds(pl.multiple_of(gy * nblk, nblk), nblk), :] = lanes
        mine = jnp.sum(acc[...].T, axis=0, keepdims=True)
        part_out[...] = jnp.broadcast_to(mine, part_out.shape)
    else:
        part_out[...] = acc[...]


def blend(index, snapshots, steps, mask, probe, part):
    stages = GROUPS[index]
    first, last = index == 0, index == len(GROUPS) - 1
    snaps, _, rows, cols = snapshots.shape
    sub = rows // 4
    n = len(stages)
    hbm, vmem = pl.BlockSpec(memory_space=pltpu.HBM), pl.BlockSpec(memory_space=pltpu.VMEM)
    args = [pltpu.with_memory_space_constraint(a, pltpu.HBM) for a in (steps, mask, probe, snapshots)]
    ins = [hbm] * 4
    if not first:
        ins.append(vmem)
        args.append(pltpu.with_memory_space_constraint(part, pltpu.VMEM))
    return pl.pallas_call(
        functools.partial(blend_kernel, stages, first, last),
        in_specs=ins,
        out_specs=[vmem] * (n + 1),
        out_shape=[pltpu.VMEM((sub, cols), jnp.bfloat16)] * n + [pltpu.VMEM((128, BLOCK), jnp.float32)],
        scratch_shapes=[
            pltpu.VMEM((n, snaps, sub, cols), jnp.float32),
            pltpu.SMEM(steps.shape, jnp.int32),
            pltpu.SMEM(mask.shape, jnp.int32),
            pltpu.VMEM(probe.shape, jnp.float32),
            pltpu.VMEM((n, sub, BLOCK), jnp.float32),
            pltpu.VMEM((128, BLOCK), jnp.float32),
            pltpu.SemaphoreType.DMA((3,)),
            pltpu.SemaphoreType.DMA((n, sub // CHUNK)),
        ],
        cost_estimate=pl.CostEstimate(
            flops=12 * n * sub * cols, bytes_accessed=n * sub * cols * (snaps * 4 + 2), transcendentals=0
        ),
        compiler_params=pltpu.CompilerParams(vmem_limit_bytes=54 << 20),
        name=f"blend{index}",
    )(*args)


def totals_kernel(parts, checks):
    t = jnp.sum(parts[...].reshape(16, 8, BLOCK), axis=0)
    checks[...] = (t[0:4] + t[4:8])[:, 0:64] / math.sqrt(4096 * BLOCK)


def totals(parts):
    return pl.pallas_call(
        totals_kernel,
        out_shape=jax.ShapeDtypeStruct((4, 64), jnp.float32),
        compiler_params=pltpu.CompilerParams(vmem_limit_bytes=54 << 20),
        name="totals",
    )(parts)


def finish_kernel(order, *refs):
    got, (out, sems) = refs[:4], refs[4:]
    gy, gz = lax.axis_index("gy"), lax.axis_index("gz")
    copies = []
    for j in range(4):
        slot = layer_from(order[j], gy, gz)
        copy = pltpu.make_async_copy(got[j], out.at[slot], sems.at[j])
        copy.start()
        copies.append(copy)
    for copy in copies:
        copy.wait()


def finish(order, got):
    sub, cols = got[0].shape
    vmem = pl.BlockSpec(memory_space=pltpu.VMEM)
    got = [pltpu.with_memory_space_constraint(g, pltpu.VMEM) for g in got]
    return pl.pallas_call(
        functools.partial(finish_kernel, order),
        in_specs=[vmem] * 4,
        out_specs=pl.BlockSpec(memory_space=pltpu.HBM),
        out_shape=jax.ShapeDtypeStruct((4, sub, cols), jnp.bfloat16),
        scratch_shapes=[pltpu.SemaphoreType.DMA((4,))],
        compiler_params=pltpu.CompilerParams(vmem_limit_bytes=54 << 20),
        name="finish",
    )(*got)


def route(shift):
    pairs = []
    for gx in range(8):
        for gy in range(4):
            for gz in range(4):
                pairs.append((gx * 16 + gy * 4 + gz, gx * 16 + STAGES[shift][gy][gz] * 4 + gy))
    return pairs


def local(snapshots, steps, mask, probe):
    probe = probe.reshape(32, BLOCK)
    part = None
    got = []
    order = sum(GROUPS, ())
    for index, shifts in enumerate(GROUPS):
        *ws, part = blend(index, snapshots, steps, mask, probe, part)
        got += [lax.ppermute(w, AXES, route(s)) for w, s in zip(ws, shifts)]
    parts = lax.all_to_all(part, AXES, 0, 0, tiled=True)
    return finish(order, got), totals(parts)


def solution(mesh):
    return jax.shard_map(
        local,
        mesh=mesh,
        in_specs=(P(None, "gz", "gx", "gy"), P(), P(), P()),
        out_specs=(P(None, ("gx", "gy"), "gz"), P()),
        check_vma=False,
    )
```

time: 57.5 us -> 43.8 us (0.76)
  Pallas kernels: 20.8 us -> 10.5 us
  blocking collectives: 24.2 us -> 17.6 us
  starting transfers between devices: 9.99 us -> 14.8 us
  local copies, waits for them, and re-layouts: 1.27 us -> 0 us
    pallas_call x5 -> x4, Pallas kernels: 20.8 us -> 10.5 us  [the longest x2 7.66 us: blend(): pl.pallas_call(functools.partial(blend_kernel, stages, first, last), in_s...]
    all_to_all x1, blocking collectives: 24.2 us -> 17.6 us  [local(): parts = lax.all_to_all(part, AXES, 0, 0, tiled=True)]
    ppermute x4, starting transfers between devices: 9.99 us -> 14.8 us  [local(): got += [lax.ppermute(w, AXES, route(s)) for w, s in zip(ws, shifts)]]
    unnamed x8 -> x0, local copies, waits for them, and re-layouts: 1.27 us -> none
  transfers between devices with their start and end apart: 4 -> 4, of which waited for: 0 -> 0; matrix products, arithmetic and copies ran while one was open for 0% -> 0% of each run, Pallas kernels for 23% -> 12%
where the time goes in v2:
time: 43.8 us; the launch traced here: 43.5 us
  blocking collectives  17.6 us (40%)
  starting transfers between devices  14.8 us (34%)
  Pallas kernels  10.5 us (24%)
  between operations  0.67 us (2%)
    all_to_all x1, blocking collectives, local(): parts = lax.all_to_all(part, AXES, 0, 0, tiled=True)  17.6 us
    ppermute x4, starting transfers between devices, local(): got += [lax.ppermute(w, AXES, route(s)) for w, s in zip(ws, shifts)]  14.8 us
    pallas_call x2, Pallas kernels, blend(): pl.pallas_call(functools.partial(blend_kernel, stages, first, last), in_s...  7.66 us
    pallas_call x1, Pallas kernels, totals(): pl.pallas_call(totals_kernel, out_shape=jax.ShapeDtypeStruct((4, 64), jnp...  1.44 us
    pallas_call x1, Pallas kernels, finish(): pl.pallas_call(functools.partial(finish_kernel, order), in_specs=[vmem] *...  1.36 us
  transfers between devices with their start and end apart: 4, of which 0 were waited for; matrix products, arithmetic and copies ran while one was open for 0% of the time, Pallas kernels for 12%

profile of v2, /device:TPU:1, one launch (start us, length us, event | category | flops | bytes accessed | tf_op | source)
XLA Modules:
  0.0 43.5 jit_solution(4808755158956076129)
XLA Ops:
  0.6 3.8 %blend0.1 = (bf16[128,2048]{1,0:T(8,128)(2,1)S(1)}, bf16[128,2048]{1,0:T(8,128)(2,1)S(1)}, f32[128,128]{1,0:T(8,128)S(1)}) custom-call(s32[4]{0:T(128)} %refs_0_.3, s32[4,64]{1,0:T(4,128)} %refs_1_.3, f32[32,128]{1,0:T(8,128)} %bitcast.7, f32[4,1,512,2048]{3,2,1,0:T(8,128)} %refs_3_.3), custom_call_target="tpu_custom_call" | custom-call | flops 6291456 | bytes 9437184 | tf_op jit(solution)/shard_map/blend0/pallas_call | solution.py:129
  4.4 3.9 %collective-permute-start = (bf16[128,2048]{1,0:T(8,128)(2,1)S(1)}, bf16[128,2048]{1,0:T(8,128)(2,1)S(1)}, u32[]{:S(2)}, u32[]{:S(2)}) collective-permute-start(bf16[128,2048]{1,0:T(8,128)(2,1)S(1)} %get-tuple-element.8), channel_id=1, source_target_pairs={{0,4},{1,12},{2,0},{3,8},{4,9},{5,1},{6,13},{7,5},{8,6},{9,14},{10... | collective-permute-start | bytes 1572872 | tf_op jit(solution)/shard_map/ppermute | solution.py:210
  8.3 0.0 collective-permute-start.1
  8.4 3.9 %blend1.1 = (bf16[128,2048]{1,0:T(8,128)(2,1)S(1)}, bf16[128,2048]{1,0:T(8,128)(2,1)S(1)}, f32[128,128]{1,0:T(8,128)S(1)}) custom-call(s32[4]{0:T(128)} %refs_0_.3, s32[4,64]{1,0:T(4,128)} %refs_1_.3, f32[32,128]{1,0:T(8,128)} %bitcast.8, f32[4,1,512,2048]{3,2,1,0:T(8,128)} %refs_3_.3, f32[128,128]{1,0:T(8,128)S(1)} %get-tuple-element.10.refs_4_), custom_call_target="tpu_custom_call" | custom-call | flops 6291456 | bytes 9437184 | tf_op jit(solution)/shard_map/blend1/pallas_call | solution.py:129
  12.2 1.9 %collective-permute-start.2 = (bf16[128,2048]{1,0:T(8,128)(2,1)S(1)}, bf16[128,2048]{1,0:T(8,128)(2,1)S(1)}, u32[]{:S(2)}, u32[]{:S(2)}) collective-permute-start(bf16[128,2048]{1,0:T(8,128)(2,1)S(1)} %get-tuple-element.11), channel_id=1, source_target_pairs={{0,12},{1,4},{2,8},{3,0},{4,1},{5,9},{6,5},{7,13},{8,14},{9,6},{10... | collective-permute-start | bytes 1572872 | tf_op jit(solution)/shard_map/ppermute | solution.py:210
  14.2 9.0 %collective-permute-start.3 = (bf16[128,2048]{1,0:T(8,128)(2,1)S(1)}, bf16[128,2048]{1,0:T(8,128)(2,1)S(1)}, u32[]{:S(2)}, u32[]{:S(2)}) collective-permute-start(bf16[128,2048]{1,0:T(8,128)(2,1)S(1)} %get-tuple-element.12), channel_id=1, source_target_pairs={{0,0},{1,8},{2,4},{3,12},{4,13},{5,5},{6,9},{7,1},{8,2},{9,10},{10... | collective-permute-start | bytes 1572872 | tf_op jit(solution)/shard_map/ppermute | solution.py:210
  23.2 17.6 %all_to_all.11 = f32[128,1,128]{2,1,0:T(1,128)} all-to-all(f32[128,1,128]{2,1,0:T(1,128)S(1)} %bitcast.5), channel_id=1, replica_groups=mesh['gx'=8,'gy'=4,'gz'=4] {'gx','gy','gz'}, dimensions={0} | all-to-all | bytes 131072 | tf_op jit(solution)/shard_map/all_to_all | solution.py:211
  40.7 1.4 %totals.1 = f32[4,64]{1,0:T(4,128)} custom-call(f32[128,128]{1,0:T(8,128)} %bitcast.6), custom_call_target="tpu_custom_call" | custom-call | tf_op jit(solution)/shard_map/totals/pallas_call | solution.py:158
  42.2 0.0 collective-permute-done.refs_0_
  42.2 0.0 collective-permute-done.1.refs_1_
  42.2 0.0 collective-permute-done.2.refs_2_
  42.2 0.0 collective-permute-done.3.refs_3_
  42.2 1.4 %finish.1 = bf16[4,128,2048]{2,1,0:T(8,128)(2,1)} custom-call(bf16[128,2048]{1,0:T(8,128)(2,1)S(1)} %collective-permute-done.refs_0_, bf16[128,2048]{1,0:T(8,128)(2,1)S(1)} %collective-permute-done.1.refs_1_, bf16[128,2048]{1,0:T(8,128)(2,1)S(1)} %collective-permute-done.2.refs_2_, bf16[128,2048]{1,0:T(8,128)(2,1)S(1)} %collective-permute-done.3.refs_3_), custom_call_target="tpu_custom_call" | custom-call | tf_op jit(solution)/shard_map/finish/pallas_call | solution.py:183
Async XLA Ops:
  4.4 37.8 %collective-permute-start = (bf16[128,2048]{1,0:T(8,128)(2,1)S(1)}, bf16[128,2048]{1,0:T(8,128)(2,1)S(1)}, u32[]{:S(2)}, u32[]{:S(2)}) collective-permute-start(bf16[128,2048]{1,0:T(8,128)(2,1)S(1)} %get-tuple-element.8), channel_id=1, source_target_pairs={{0,4},{1,12},{2,0},{3,8},{4,9},{5,1},{6,13},{7,5},{8,6},{9,14},{10... | collective-permute-start | bytes 1572872 | tf_op jit(solution)/shard_map/ppermute | solution.py:210
  8.3 33.8 %collective-permute-start.1 = (bf16[128,2048]{1,0:T(8,128)(2,1)S(1)}, bf16[128,2048]{1,0:T(8,128)(2,1)S(1)}, u32[]{:S(2)}, u32[]{:S(2)}) collective-permute-start(bf16[128,2048]{1,0:T(8,128)(2,1)S(1)} %get-tuple-element.9), channel_id=1, source_target_pairs={{0,8},{1,0},{2,12},{3,4},{4,5},{5,13},{6,1},{7,9},{8,10},{9,2},{10... | collective-permute-start | bytes 1572872 | tf_op jit(solution)/shard_map/ppermute | solution.py:210
  12.2 29.9 %collective-permute-start.2 = (bf16[128,2048]{1,0:T(8,128)(2,1)S(1)}, bf16[128,2048]{1,0:T(8,128)(2,1)S(1)}, u32[]{:S(2)}, u32[]{:S(2)}) collective-permute-start(bf16[128,2048]{1,0:T(8,128)(2,1)S(1)} %get-tuple-element.11), channel_id=1, source_target_pairs={{0,12},{1,4},{2,8},{3,0},{4,1},{5,9},{6,5},{7,13},{8,14},{9,6},{10... | collective-permute-start | bytes 1572872 | tf_op jit(solution)/shard_map/ppermute | solution.py:210
  14.2 28.0 %collective-permute-start.3 = (bf16[128,2048]{1,0:T(8,128)(2,1)S(1)}, bf16[128,2048]{1,0:T(8,128)(2,1)S(1)}, u32[]{:S(2)}, u32[]{:S(2)}) collective-permute-start(bf16[128,2048]{1,0:T(8,128)(2,1)S(1)} %get-tuple-element.12), channel_id=1, source_target_pairs={{0,0},{1,8},{2,4},{3,12},{4,13},{5,5},{6,9},{7,1},{8,2},{9,10},{10... | collective-permute-start | bytes 1572872 | tf_op jit(solution)/shard_map/ppermute | solution.py:210

commit v3 on v2

--- a/solution.py
+++ b/solution.py
@@ -6,13 +6,15 @@
 from jax import lax
 from jax.experimental import pallas as pl
 from jax.experimental.pallas import tpu as pltpu
+from jax.sharding import Mesh
 from jax.sharding import PartitionSpec as P
+
 
 BLOCK = 128
 DECAY_SPAN = 1000.0
 GROUPS = ((0, 1), (2, 3))
 CHUNK = 32
-AXES = ("gx", "gy", "gz")
+AXES = ("ylo", "z", "gy", "yhi", "core")
 STAGES = (
     ((1, 3, 0, 2), (2, 0, 3, 1), (1, 3, 0, 2), (2, 0, 3, 1)),
     ((2, 0, 3, 1), (1, 3, 0, 2), (2, 0, 3, 1), (1, 3, 0, 2)),
@@ -25,6 +27,11 @@
     packed = sum(table[m][n] << (2 * (4 * m + n)) for m in range(4) for n in range(4))
     packed = packed - (1 << 32) if packed >= 1 << 31 else packed
     return jnp.bitwise_and(lax.shift_right_logical(jnp.int32(packed), (4 * i + j) * 2), 3)
+
+
+def place():
+    ylo, z, gy, yhi, core = (lax.axis_index(a) for a in AXES)
+    return ylo * 4 + z, gy, yhi * 2 + core
 
 
 def sent_to(stage, gy, gz):
@@ -46,7 +53,7 @@
     nblk = x_hbm.shape[3] // BLOCK
     sub = x_hbm.shape[2] // 4
     per = sub // CHUNK
-    gx, gy, gz = (lax.axis_index(a) for a in AXES)
+    gx, gy, gz = place()
     quarter = [sent_to(s, gy, gz) for s in stages]
 
     tables = [
@@ -107,7 +114,8 @@
     if last:
         lanes = jnp.sum(acc[...].reshape(nblk, 8, BLOCK), axis=1)
         acc[...] = jnp.zeros_like(acc)
-        acc[pl.ds(pl.multiple_of(gy * nblk, nblk), nblk), :] = lanes
+        spot = lax.axis_index("yhi") * 4 + gy
+        acc[pl.ds(pl.multiple_of(spot * nblk, nblk), nblk), :] = lanes
         mine = jnp.sum(acc[...].T, axis=0, keepdims=True)
         part_out[...] = jnp.broadcast_to(mine, part_out.shape)
     else:
@@ -144,28 +152,30 @@
         cost_estimate=pl.CostEstimate(
             flops=12 * n * sub * cols, bytes_accessed=n * sub * cols * (snaps * 4 + 2), transcendentals=0
         ),
-        compiler_params=pltpu.CompilerParams(vmem_limit_bytes=54 << 20),
-        name=f"blend{index}",
+        compiler_params=pltpu.CompilerParams(vmem_limit_bytes=49 << 20),
     )(*args)
 
 
 def totals_kernel(parts, checks):
+    half = checks.shape[1]
     t = jnp.sum(parts[...].reshape(16, 8, BLOCK), axis=0)
-    checks[...] = (t[0:4] + t[4:8])[:, 0:64] / math.sqrt(4096 * BLOCK)
+    t = ((t[0:2] + t[2:4]) + (t[4:6] + t[6:8])) / math.sqrt(4096 * BLOCK)
+    checks[0:2] = t[:, :half]
+    checks[2:4] = t[:, half:]
 
 
 def totals(parts):
     return pl.pallas_call(
         totals_kernel,
         out_shape=jax.ShapeDtypeStruct((4, 64), jnp.float32),
-        compiler_params=pltpu.CompilerParams(vmem_limit_bytes=54 << 20),
+        compiler_params=pltpu.CompilerParams(vmem_limit_bytes=4 << 20),
         name="totals",
     )(parts)
 
 
 def finish_kernel(order, *refs):
     got, (out, sems) = refs[:4], refs[4:]
-    gy, gz = lax.axis_index("gy"), lax.axis_index("gz")
+    _, gy, gz = place()
     copies = []
     for j in range(4):
         slot = layer_from(order[j], gy, gz)
@@ -186,7 +196,7 @@
         out_specs=pl.BlockSpec(memory_space=pltpu.HBM),
         out_shape=jax.ShapeDtypeStruct((4, sub, cols), jnp.bfloat16),
         scratch_shapes=[pltpu.SemaphoreType.DMA((4,))],
-        compiler_params=pltpu.CompilerParams(vmem_limit_bytes=54 << 20),
+        compiler_params=pltpu.CompilerParams(vmem_limit_bytes=4 << 20),
         name="finish",
     )(*got)
 
@@ -200,23 +210,34 @@
     return pairs
 
 
-def local(snapshots, steps, mask, probe):
+def exchange(ws, stages):
+    moved = []
+    for w, s in zip(ws, stages):
+        moved.append(lax.ppermute(w, AXES, route(s)))
+    return moved
+
+
+def gather_checks(part):
+    return totals(lax.all_to_all(part, AXES, 0, 0, tiled=True))
+
+
+def consolidate(snapshots, steps, mask, probe):
     probe = probe.reshape(32, BLOCK)
     part = None
     got = []
-    order = sum(GROUPS, ())
-    for index, shifts in enumerate(GROUPS):
+    for index, stages in enumerate(GROUPS):
         *ws, part = blend(index, snapshots, steps, mask, probe, part)
-        got += [lax.ppermute(w, AXES, route(s)) for w, s in zip(ws, shifts)]
-    parts = lax.all_to_all(part, AXES, 0, 0, tiled=True)
-    return finish(order, got), totals(parts)
+        got += exchange(ws, stages)
+    checks = gather_checks(part)
+    return finish(sum(GROUPS, ()), got), checks
 
 
 def solution(mesh):
+    split = Mesh(mesh.devices.reshape(2, 4, 4, 2, 2), AXES)
     return jax.shard_map(
-        local,
-        mesh=mesh,
-        in_specs=(P(None, "gz", "gx", "gy"), P(), P(), P()),
-        out_specs=(P(None, ("gx", "gy"), "gz"), P()),
+        consolidate,
+        mesh=split,
+        in_specs=(P(None, ("yhi", "core"), ("ylo", "z"), "gy"), P(), P(), P()),
+        out_specs=(P(None, ("ylo", "z", "gy"), ("yhi", "core")), P()),
         check_vma=False,
     )

time: 43.8 us -> 42.5 us (0.970)
  Pallas kernels: 10.5 us -> 9.7 us
  blocking collectives: 17.6 us -> 17.1 us
    pallas_call x1, Pallas kernels: 1.44 us -> 0.67 us  [totals(): pl.pallas_call(totals_kernel, out_shape=jax.ShapeDtypeStruct((4, 64), jnp...]
    all_to_all x1, blocking collectives: 17.6 us -> 17.1 us  [gather_checks(): return totals(lax.all_to_all(part, AXES, 0, 0, tiled=True))]
  transfers between devices with their start and end apart: 4 -> 4, of which waited for: 0 -> 0; matrix products, arithmetic and copies ran while one was open for 0% -> 0% of each run, Pallas kernels for 12% -> 11%
where the time goes in v3:
time: 42.5 us; the launch traced here: 42.3 us
  blocking collectives  17.1 us (40%)
  starting transfers between devices  14.8 us (35%)
  Pallas kernels  9.7 us (23%)
  between operations  0.67 us (2%)
    all_to_all x1, blocking collectives, gather_checks(): return totals(lax.all_to_all(part, AXES, 0, 0, tiled=True))  17.1 us
    ppermute x4, starting transfers between devices, exchange(): moved.append(lax.ppermute(w, AXES, route(s)))  14.8 us
    pallas_call x2, Pallas kernels, blend(): pl.pallas_call(functools.partial(blend_kernel, stages, first, last), in_s...  7.67 us
    pallas_call x1, Pallas kernels, finish(): pl.pallas_call(functools.partial(finish_kernel, order), in_specs=[vmem] *...  1.36 us
  transfers between devices with their start and end apart: 4, of which 0 were waited for; matrix products, arithmetic and copies ran while one was open for 0% of the time, Pallas kernels for 11%

profile of v3, /device:TPU:1, one launch (start us, length us, event | category | flops | bytes accessed | tf_op | source)
XLA Modules:
  0.0 42.3 jit_solution(14642722363449722633)
XLA Ops:
  0.6 3.8 %shard_map.59 = (bf16[128,2048]{1,0:T(8,128)(2,1)S(1)}, bf16[128,2048]{1,0:T(8,128)(2,1)S(1)}, f32[128,128]{1,0:T(8,128)S(1)}) custom-call(s32[4]{0:T(128)} %refs_0_.3, s32[4,64]{1,0:T(4,128)} %refs_1_.3, f32[32,128]{1,0:T(8,128)} %bitcast.7, f32[4,1,512,2048]{3,2,1,0:T(8,128)} %refs_3_.3), custom_call_target="tpu_custom_call" | custom-call | flops 6291456 | bytes 9437184 | tf_op jit(solution)/shard_map/pallas_call | solution.py:137
  4.4 3.9 %collective-permute-start = (bf16[128,2048]{1,0:T(8,128)(2,1)S(1)}, bf16[128,2048]{1,0:T(8,128)(2,1)S(1)}, u32[]{:S(2)}, u32[]{:S(2)}) collective-permute-start(bf16[128,2048]{1,0:T(8,128)(2,1)S(1)} %get-tuple-element.8), channel_id=1, source_target_pairs={{0,4},{1,12},{2,0},{3,8},{4,9},{5,1},{6,13},{7,5},{8,6},{9,14},{10... | collective-permute-start | bytes 1572872 | tf_op jit(solution)/shard_map/ppermute | solution.py:216
  8.4 0.0 collective-permute-start.1
  8.4 3.9 %shard_map.60 = (bf16[128,2048]{1,0:T(8,128)(2,1)S(1)}, bf16[128,2048]{1,0:T(8,128)(2,1)S(1)}, f32[128,128]{1,0:T(8,128)S(1)}) custom-call(s32[4]{0:T(128)} %refs_0_.3, s32[4,64]{1,0:T(4,128)} %refs_1_.3, f32[32,128]{1,0:T(8,128)} %bitcast.8, f32[4,1,512,2048]{3,2,1,0:T(8,128)} %refs_3_.3, f32[128,128]{1,0:T(8,128)S(1)} %get-tuple-element.10.refs_4_), custom_call_target="tpu_custom_call" | custom-call | flops 6291456 | bytes 9437184 | tf_op jit(solution)/shard_map/pallas_call | solution.py:137
  12.3 1.9 %collective-permute-start.2 = (bf16[128,2048]{1,0:T(8,128)(2,1)S(1)}, bf16[128,2048]{1,0:T(8,128)(2,1)S(1)}, u32[]{:S(2)}, u32[]{:S(2)}) collective-permute-start(bf16[128,2048]{1,0:T(8,128)(2,1)S(1)} %get-tuple-element.11), channel_id=1, source_target_pairs={{0,12},{1,4},{2,8},{3,0},{4,1},{5,9},{6,5},{7,13},{8,14},{9,6},{10... | collective-permute-start | bytes 1572872 | tf_op jit(solution)/shard_map/ppermute | solution.py:216
  14.2 9.0 %collective-permute-start.3 = (bf16[128,2048]{1,0:T(8,128)(2,1)S(1)}, bf16[128,2048]{1,0:T(8,128)(2,1)S(1)}, u32[]{:S(2)}, u32[]{:S(2)}) collective-permute-start(bf16[128,2048]{1,0:T(8,128)(2,1)S(1)} %get-tuple-element.12), channel_id=1, source_target_pairs={{0,0},{1,8},{2,4},{3,12},{4,13},{5,5},{6,9},{7,1},{8,2},{9,10},{10... | collective-permute-start | bytes 1572872 | tf_op jit(solution)/shard_map/ppermute | solution.py:216
  23.2 17.1 %all_to_all.11 = f32[128,1,128]{2,1,0:T(1,128)S(1)} all-to-all(f32[128,1,128]{2,1,0:T(1,128)S(1)} %bitcast.6), channel_id=1, replica_groups=mesh['ylo'=2,'z'=4,'gy'=4,'yhi'=2,'core'=2] {'ylo','z','gy','yhi','core'}, dimensions={0} | all-to-all | bytes 131072 | tf_op jit(solution)/shard_map/all_to_all | solution.py:221
  40.2 0.7 %totals.1 = f32[4,64]{1,0:T(4,128)} custom-call(f32[128,128]{1,0:T(8,128)S(1)} %bitcast.5), custom_call_target="tpu_custom_call" | custom-call | tf_op jit(solution)/shard_map/totals/pallas_call | solution.py:168
  40.9 0.0 collective-permute-done.refs_0_
  40.9 0.0 collective-permute-done.1.refs_1_
  40.9 0.0 collective-permute-done.2.refs_2_
  40.9 0.0 collective-permute-done.3.refs_3_
  40.9 1.4 %finish.1 = bf16[4,128,2048]{2,1,0:T(8,128)(2,1)} custom-call(bf16[128,2048]{1,0:T(8,128)(2,1)S(1)} %collective-permute-done.refs_0_, bf16[128,2048]{1,0:T(8,128)(2,1)S(1)} %collective-permute-done.1.refs_1_, bf16[128,2048]{1,0:T(8,128)(2,1)S(1)} %collective-permute-done.2.refs_2_, bf16[128,2048]{1,0:T(8,128)(2,1)S(1)} %collective-permute-done.3.refs_3_), custom_call_target="tpu_custom_call" | custom-call | tf_op jit(solution)/shard_map/finish/pallas_call | solution.py:193
Async XLA Ops:
  4.4 36.5 %collective-permute-start = (bf16[128,2048]{1,0:T(8,128)(2,1)S(1)}, bf16[128,2048]{1,0:T(8,128)(2,1)S(1)}, u32[]{:S(2)}, u32[]{:S(2)}) collective-permute-start(bf16[128,2048]{1,0:T(8,128)(2,1)S(1)} %get-tuple-element.8), channel_id=1, source_target_pairs={{0,4},{1,12},{2,0},{3,8},{4,9},{5,1},{6,13},{7,5},{8,6},{9,14},{10... | collective-permute-start | bytes 1572872 | tf_op jit(solution)/shard_map/ppermute | solution.py:216
  8.4 32.6 %collective-permute-start.1 = (bf16[128,2048]{1,0:T(8,128)(2,1)S(1)}, bf16[128,2048]{1,0:T(8,128)(2,1)S(1)}, u32[]{:S(2)}, u32[]{:S(2)}) collective-permute-start(bf16[128,2048]{1,0:T(8,128)(2,1)S(1)} %get-tuple-element.9), channel_id=1, source_target_pairs={{0,8},{1,0},{2,12},{3,4},{4,5},{5,13},{6,1},{7,9},{8,10},{9,2},{10... | collective-permute-start | bytes 1572872 | tf_op jit(solution)/shard_map/ppermute | solution.py:216
  12.3 28.7 %collective-permute-start.2 = (bf16[128,2048]{1,0:T(8,128)(2,1)S(1)}, bf16[128,2048]{1,0:T(8,128)(2,1)S(1)}, u32[]{:S(2)}, u32[]{:S(2)}) collective-permute-start(bf16[128,2048]{1,0:T(8,128)(2,1)S(1)} %get-tuple-element.11), channel_id=1, source_target_pairs={{0,12},{1,4},{2,8},{3,0},{4,1},{5,9},{6,5},{7,13},{8,14},{9,6},{10... | collective-permute-start | bytes 1572872 | tf_op jit(solution)/shard_map/ppermute | solution.py:216
  14.2 26.7 %collective-permute-start.3 = (bf16[128,2048]{1,0:T(8,128)(2,1)S(1)}, bf16[128,2048]{1,0:T(8,128)(2,1)S(1)}, u32[]{:S(2)}, u32[]{:S(2)}) collective-permute-start(bf16[128,2048]{1,0:T(8,128)(2,1)S(1)} %get-tuple-element.12), channel_id=1, source_target_pairs={{0,0},{1,8},{2,4},{3,12},{4,13},{5,5},{6,9},{7,1},{8,2},{9,10},{10... | collective-permute-start | bytes 1572872 | tf_op jit(solution)/shard_map/ppermute | solution.py:216

commit v4 on v3

--- a/solution.py
+++ b/solution.py
@@ -16,10 +16,10 @@
 CHUNK = 32
 AXES = ("ylo", "z", "gy", "yhi", "core")
 STAGES = (
-    ((1, 3, 0, 2), (2, 0, 3, 1), (1, 3, 0, 2), (2, 0, 3, 1)),
-    ((2, 0, 3, 1), (1, 3, 0, 2), (2, 0, 3, 1), (1, 3, 0, 2)),
-    ((3, 1, 2, 0), (0, 2, 1, 3), (3, 1, 2, 0), (0, 2, 1, 3)),
-    ((0, 2, 1, 3), (3, 1, 2, 0), (0, 2, 1, 3), (3, 1, 2, 0)),
+    ((1, 3, 2, 0), (2, 0, 3, 1), (1, 3, 0, 2), (0, 2, 3, 1)),
+    ((2, 0, 1, 3), (1, 3, 0, 2), (2, 0, 1, 3), (3, 1, 2, 0)),
+    ((3, 1, 0, 2), (0, 2, 1, 3), (3, 1, 2, 0), (2, 0, 1, 3)),
+    ((0, 2, 3, 1), (3, 1, 2, 0), (0, 2, 3, 1), (1, 3, 0, 2)),
 )
 
 

time: 42.5 us -> 43.4 us (1.021)
  blocking collectives: 17.1 us -> 20 us
  starting transfers between devices: 14.8 us -> 12.8 us
    all_to_all x1, blocking collectives: 17.1 us -> 20 us  [gather_checks(): return totals(lax.all_to_all(part, AXES, 0, 0, tiled=True))]
    ppermute x4, starting transfers between devices: 14.8 us -> 12.8 us  [exchange(): moved.append(lax.ppermute(w, AXES, route(s)))]
where the time goes in v4:
time: 43.4 us; the launch traced here: 43.2 us
  blocking collectives  20 us (46%)
  starting transfers between devices  12.8 us (29%)
  Pallas kernels  9.7 us (22%)
  between operations  0.67 us (2%)
    all_to_all x1, blocking collectives, gather_checks(): return totals(lax.all_to_all(part, AXES, 0, 0, tiled=True))  20 us
    ppermute x4, starting transfers between devices, exchange(): moved.append(lax.ppermute(w, AXES, route(s)))  12.8 us
    pallas_call x2, Pallas kernels, blend(): pl.pallas_call(functools.partial(blend_kernel, stages, first, last), in_s...  7.67 us
    pallas_call x1, Pallas kernels, finish(): pl.pallas_call(functools.partial(finish_kernel, order), in_specs=[vmem] *...  1.36 us
  transfers between devices with their start and end apart: 4, of which 0 were waited for; matrix products, arithmetic and copies ran while one was open for 0% of the time, Pallas kernels for 11%

profile of v4, /device:TPU:1, one launch (start us, length us, event | category | flops | bytes accessed | tf_op | source)
XLA Modules:
  0.0 43.2 jit_solution(10335416049489370747)
XLA Ops:
  0.6 3.8 %shard_map.59 = (bf16[128,2048]{1,0:T(8,128)(2,1)S(1)}, bf16[128,2048]{1,0:T(8,128)(2,1)S(1)}, f32[128,128]{1,0:T(8,128)S(1)}) custom-call(s32[4]{0:T(128)} %refs_0_.3, s32[4,64]{1,0:T(4,128)} %refs_1_.3, f32[32,128]{1,0:T(8,128)} %bitcast.7, f32[4,1,512,2048]{3,2,1,0:T(8,128)} %refs_3_.3), custom_call_target="tpu_custom_call" | custom-call | flops 6291456 | bytes 9437184 | tf_op jit(solution)/shard_map/pallas_call | solution.py:137
  4.4 3.9 %collective-permute-start = (bf16[128,2048]{1,0:T(8,128)(2,1)S(1)}, bf16[128,2048]{1,0:T(8,128)(2,1)S(1)}, u32[]{:S(2)}, u32[]{:S(2)}) collective-permute-start(bf16[128,2048]{1,0:T(8,128)(2,1)S(1)} %get-tuple-element.8), channel_id=1, source_target_pairs={{0,4},{1,12},{2,8},{3,0},{4,9},{5,1},{6,13},{7,5},{8,6},{9,14},{10... | collective-permute-start | bytes 1572872 | tf_op jit(solution)/shard_map/ppermute | solution.py:216
  8.4 0.0 collective-permute-start.1
  8.4 3.9 %shard_map.60 = (bf16[128,2048]{1,0:T(8,128)(2,1)S(1)}, bf16[128,2048]{1,0:T(8,128)(2,1)S(1)}, f32[128,128]{1,0:T(8,128)S(1)}) custom-call(s32[4]{0:T(128)} %refs_0_.3, s32[4,64]{1,0:T(4,128)} %refs_1_.3, f32[32,128]{1,0:T(8,128)} %bitcast.8, f32[4,1,512,2048]{3,2,1,0:T(8,128)} %refs_3_.3, f32[128,128]{1,0:T(8,128)S(1)} %get-tuple-element.10.refs_4_), custom_call_target="tpu_custom_call" | custom-call | flops 6291456 | bytes 9437184 | tf_op jit(solution)/shard_map/pallas_call | solution.py:137
  12.3 1.9 %collective-permute-start.2 = (bf16[128,2048]{1,0:T(8,128)(2,1)S(1)}, bf16[128,2048]{1,0:T(8,128)(2,1)S(1)}, u32[]{:S(2)}, u32[]{:S(2)}) collective-permute-start(bf16[128,2048]{1,0:T(8,128)(2,1)S(1)} %get-tuple-element.11), channel_id=1, source_target_pairs={{0,12},{1,4},{2,0},{3,8},{4,1},{5,9},{6,5},{7,13},{8,14},{9,6},{10... | collective-permute-start | bytes 1572872 | tf_op jit(solution)/shard_map/ppermute | solution.py:216
  14.2 6.9 %collective-permute-start.3 = (bf16[128,2048]{1,0:T(8,128)(2,1)S(1)}, bf16[128,2048]{1,0:T(8,128)(2,1)S(1)}, u32[]{:S(2)}, u32[]{:S(2)}) collective-permute-start(bf16[128,2048]{1,0:T(8,128)(2,1)S(1)} %get-tuple-element.12), channel_id=1, source_target_pairs={{0,0},{1,8},{2,12},{3,4},{4,13},{5,5},{6,9},{7,1},{8,2},{9,10},{10... | collective-permute-start | bytes 1572872 | tf_op jit(solution)/shard_map/ppermute | solution.py:216
  21.1 20.0 %all_to_all.11 = f32[128,1,128]{2,1,0:T(1,128)S(1)} all-to-all(f32[128,1,128]{2,1,0:T(1,128)S(1)} %bitcast.6), channel_id=1, replica_groups=mesh['ylo'=2,'z'=4,'gy'=4,'yhi'=2,'core'=2] {'ylo','z','gy','yhi','core'}, dimensions={0} | all-to-all | bytes 131072 | tf_op jit(solution)/shard_map/all_to_all | solution.py:221
  41.2 0.7 %totals.1 = f32[4,64]{1,0:T(4,128)} custom-call(f32[128,128]{1,0:T(8,128)S(1)} %bitcast.5), custom_call_target="tpu_custom_call" | custom-call | tf_op jit(solution)/shard_map/totals/pallas_call | solution.py:168
  41.8 0.0 collective-permute-done.refs_0_
  41.8 0.0 collective-permute-done.1.refs_1_
  41.8 0.0 collective-permute-done.2.refs_2_
  41.8 0.0 collective-permute-done.3.refs_3_
  41.8 1.4 %finish.1 = bf16[4,128,2048]{2,1,0:T(8,128)(2,1)} custom-call(bf16[128,2048]{1,0:T(8,128)(2,1)S(1)} %collective-permute-done.refs_0_, bf16[128,2048]{1,0:T(8,128)(2,1)S(1)} %collective-permute-done.1.refs_1_, bf16[128,2048]{1,0:T(8,128)(2,1)S(1)} %collective-permute-done.2.refs_2_, bf16[128,2048]{1,0:T(8,128)(2,1)S(1)} %collective-permute-done.3.refs_3_), custom_call_target="tpu_custom_call" | custom-call | tf_op jit(solution)/shard_map/finish/pallas_call | solution.py:193
Async XLA Ops:
  4.4 37.4 %collective-permute-start = (bf16[128,2048]{1,0:T(8,128)(2,1)S(1)}, bf16[128,2048]{1,0:T(8,128)(2,1)S(1)}, u32[]{:S(2)}, u32[]{:S(2)}) collective-permute-start(bf16[128,2048]{1,0:T(8,128)(2,1)S(1)} %get-tuple-element.8), channel_id=1, source_target_pairs={{0,4},{1,12},{2,8},{3,0},{4,9},{5,1},{6,13},{7,5},{8,6},{9,14},{10... | collective-permute-start | bytes 1572872 | tf_op jit(solution)/shard_map/ppermute | solution.py:216
  8.4 33.5 %collective-permute-start.1 = (bf16[128,2048]{1,0:T(8,128)(2,1)S(1)}, bf16[128,2048]{1,0:T(8,128)(2,1)S(1)}, u32[]{:S(2)}, u32[]{:S(2)}) collective-permute-start(bf16[128,2048]{1,0:T(8,128)(2,1)S(1)} %get-tuple-element.9), channel_id=1, source_target_pairs={{0,8},{1,0},{2,4},{3,12},{4,5},{5,13},{6,1},{7,9},{8,10},{9,2},{10... | collective-permute-start | bytes 1572872 | tf_op jit(solution)/shard_map/ppermute | solution.py:216
  12.3 29.6 %collective-permute-start.2 = (bf16[128,2048]{1,0:T(8,128)(2,1)S(1)}, bf16[128,2048]{1,0:T(8,128)(2,1)S(1)}, u32[]{:S(2)}, u32[]{:S(2)}) collective-permute-start(bf16[128,2048]{1,0:T(8,128)(2,1)S(1)} %get-tuple-element.11), channel_id=1, source_target_pairs={{0,12},{1,4},{2,0},{3,8},{4,1},{5,9},{6,5},{7,13},{8,14},{9,6},{10... | collective-permute-start | bytes 1572872 | tf_op jit(solution)/shard_map/ppermute | solution.py:216
  14.2 27.7 %collective-permute-start.3 = (bf16[128,2048]{1,0:T(8,128)(2,1)S(1)}, bf16[128,2048]{1,0:T(8,128)(2,1)S(1)}, u32[]{:S(2)}, u32[]{:S(2)}) collective-permute-start(bf16[128,2048]{1,0:T(8,128)(2,1)S(1)} %get-tuple-element.12), channel_id=1, source_target_pairs={{0,0},{1,8},{2,12},{3,4},{4,13},{5,5},{6,9},{7,1},{8,2},{9,10},{10... | collective-permute-start | bytes 1572872 | tf_op jit(solution)/shard_map/ppermute | solution.py:216
